TPU v7x, 32 devices: a whole 2x2x4 slice. The times are simulated.
32 devices in a mesh: gx: 8 (over y, x, core), gy: 4 (over z).
Axes of the slice: x: 2, y: 2, z: 4, core: 2. Of those that a mesh axis runs over, the one named last changes fastest.
Arguments:
- ocean_heat_field: float32 [8, 192, 128, 128], P('gy', 'gx'), may hold values from -6 to 6
- patch_zone: int32 [192], replicated, may hold values from 0 to 31, as said below
- patch_position: int32 [192], replicated, may hold values from 0 to 11, as said below
- quarter_spins: int32 [192], replicated, may hold values from 0 to 3
- zone_patch_tally: int32 [32], P(('gx', 'gy')), may hold values from 0 to 12, as said below
Outputs:
- regional: float32 [8, 32, 12, 128, 128], P(None, ('gx', 'gy'))
Inputs may be any that keep to these rules, and one draw needn't show every extreme that they name: In each aligned group of 24 blocks no more than 6 go to regions of one column patch_zone // 4, and each group has a column with exactly 6. A region receives at most 12 blocks and some region receives exactly 12. `patch_position`: the blocks of one region have distinct slots 0 to zone_patch_tally of that region minus 1, in increasing block order. zone_patch_tally[r] is the number of blocks j with patch_zone[j] = r.
All inputs are finite; a program needn't handle non-finite values.
Results may differ from a plain program's by a relative error of at most 0.00002.
Values sent between devices are 32-bit elements; how exact they have to be, the bound alone decides.
A program may use at most 128 MiB of HBM per device.

v0:
```python
import jax
import jax.numpy as jnp
from jax import lax
from jax.sharding import PartitionSpec as P


def spin_patches(incoming_patches, turn_codes):
    first_turn = jnp.rot90(incoming_patches, 1, axes=(2, 3))
    half_turn = jnp.rot90(incoming_patches, 2, axes=(2, 3))
    last_turn = jnp.rot90(incoming_patches, 3, axes=(2, 3))
    shaped = turn_codes[None, :, None, None]
    return jnp.where(
        shaped == 0,
        incoming_patches,
        jnp.where(shaped == 1, first_turn, jnp.where(shaped == 2, half_turn, last_turn)),
    )


def rank_within(labels, label_count):
    onehot = (labels[:, None] == jnp.arange(label_count, dtype=jnp.int32)[None, :]).astype(
        jnp.int32
    )
    running = jnp.cumsum(onehot, axis=0) - onehot
    return jnp.sum(running * onehot, axis=1)


def on_device(ocean_heat_field, patch_zone, patch_position, quarter_spins, zone_patch_tally):
    epoch_anomalies = ocean_heat_field.shape[0]
    patch_anomalies = ocean_heat_field.shape[1]
    patch_side_length = ocean_heat_field.shape[2]
    column_count = lax.axis_size("gx")
    row_count = lax.axis_size("gy")
    block_total = patch_zone.shape[0]
    per_peer = 2 * patch_anomalies // column_count
    capacity = 2 * patch_anomalies // row_count
    column = patch_zone // row_count
    block_ids = jnp.arange(block_total, dtype=jnp.int32)
    source_group = block_ids // patch_anomalies
    order_rank = rank_within(source_group * column_count + column, column_count * column_count)
    send_place = column * per_peer + order_rank
    my_column = lax.axis_index("gx")
    first_block = my_column * patch_anomalies
    mine_place = lax.dynamic_slice_in_dim(send_place, first_block, patch_anomalies)
    mine_turns = lax.dynamic_slice_in_dim(quarter_spins, first_block, patch_anomalies)
    incoming_patches = ocean_heat_field
    incoming_patches = spin_patches(incoming_patches, mine_turns)
    outgoing = jnp.zeros(
        (epoch_anomalies, column_count * per_peer, patch_side_length, patch_side_length),
        jnp.float32,
    )
    outgoing = outgoing.at[:, mine_place].set(incoming_patches)
    arrived = lax.all_to_all(outgoing, "gx", split_axis=1, concat_axis=1, tiled=True)
    arrival = source_group * per_peer + order_rank
    row_ids = jnp.arange(row_count, dtype=jnp.int32)[:, None]
    slot_ids = jnp.arange(capacity, dtype=jnp.int32)[None, :]
    targets = ((my_column * row_count + row_ids) * capacity + slot_ids).reshape(-1)
    flat_dest = patch_zone * capacity + patch_position
    matched = flat_dest[None, :] == targets[:, None]
    source = jnp.sum(jnp.where(matched, arrival[None, :] + 1, 0), axis=1) - 1
    present = source >= 0
    picked = jnp.take(arrived, jnp.maximum(source, 0), axis=1)
    picked = jnp.where(present[None, :, None, None], picked, jnp.float32(0.0))
    regional = lax.all_to_all(picked, "gy", split_axis=1, concat_axis=0, tiled=True)
    in_use = jnp.arange(capacity, dtype=jnp.int32) < zone_patch_tally[0]
    regional = jnp.where(in_use[None, :, None, None], regional, jnp.float32(0.0))
    regional = regional - jnp.mean(regional, axis=0, keepdims=True)
    return regional[:, None]


def solution(mesh):
    placed = (P("gy", "gx", None, None), P(), P(), P(), P(("gx", "gy")))
    return jax.shard_map(
        on_device,
        mesh=mesh,
        in_specs=placed,
        out_specs=P(None, ("gx", "gy"), None, None, None),
        check_vma=False,
    )
```

profile of v0, /device:TPU:2, one launch (start us, length us, event | category | flops | bytes accessed | tf_op | source)
XLA Modules:
  0.0 334.6 jit_solution(8710687670302286173)
XLA Ops:
  0.0 2.4 copy.42
  2.4 25.7 %rev.17 = f32[2,24,128,128]{3,2,1,0:T(8,128)} reverse(f32[2,24,128,128]{3,2,1,0:T(8,128)} %param.5), dimensions={2,3} | reverse | bytes 6291456 | tf_op jit(solution)/shard_map/jit(rot90)/jit(_flip)/rev | solution.py:9
  28.1 0.0 copy-start.2
  28.1 15.3 %rev.16 = f32[2,24,128,128]{2,3,1,0:T(8,128)} reverse(f32[2,24,128,128]{2,3,1,0:T(8,128)S(1)} %copy.42), dimensions={3} | reverse | bytes 6291456 | tf_op jit(solution)/shard_map/jit(rot90)/jit(_flip)/rev | solution.py:8
  43.4 17.0 %rev.18 = f32[2,24,128,128]{3,2,1,0:T(8,128)} reverse(f32[2,24,128,128]{3,2,1,0:T(8,128)S(1)} %bitcast.34), dimensions={3} | reverse | bytes 6291456 | tf_op jit(solution)/shard_map/jit(rot90)/jit(_flip)/rev | solution.py:10
  60.4 0.0 copy-done.2
  60.4 0.1 broadcast_compare_fusion.2
  60.5 6.2 %fusion.2 = f32[24,2,128,128]{3,2,0,1:T(8,128)S(1)} fusion(f32[2,24,128,128]{3,2,1,0:T(8,128)} %param.5, f32[2,24,128,128]{2,3,1,0:T(8,128)} %rev.16, f32[2,24,128,128]{3,2,1,0:T(8,128)} %rev.17, f32[2,24,128,128]{3,2,1,0:T(8,128)} %rev.18, pred[24]{0:T(512)(128)(4,1)S(1)} %get-tuple-element.12, pred[24]{0:T(512)(128)(4,1)S(1)} %get-tuple-element.11, ...), kind=kLoop, calls=%fused_computation.8 | loop fusion | flops 2359296 | bytes 15728712 | tf_op jit(solution)/shard_map/jit(_where)/select_n | solution.py:12
  66.7 0.0 copy-start
  66.7 0.0 copy-start.1
  66.7 0.2 copy.44
  66.9 0.4 copy-done
  67.4 0.0 copy-done.1
  67.4 0.6 reduce-window.6
  68.0 0.2 slice_reduce_fusion
  68.3 0.1 bitcast_bitcast_fusion
  68.4 0.1 compare_select_fusion
  68.5 3.5 %broadcast_in_dim.88 = f32[2,48,128,128]{3,2,1,0:T(8,128)} broadcast(f32[]{:T(128)} %constant.72.clone.1), dimensions={} | broadcast | bytes 6291460 | tf_op jit(solution)/shard_map/broadcast_in_dim | solution.py:47
  72.0 6.4 %scatter_fusion = f32[2,48,128,128]{3,2,1,0:T(8,128)} fusion(f32[2,48,128,128]{3,2,1,0:T(8,128)} %broadcast_in_dim.88, s32[24]{0:T(128)S(1)} %compare_select_fusion, f32[24,2,128,128]{3,2,1,0:T(8,128)S(1)} %copy.44), kind=kCustom, calls=%fused_computation.1 | custom fusion | bytes 9437280 | tf_op jit(solution)/shard_map/scatter | solution.py:51
  78.4 6.2 %copy.45 = f32[2,48,128,128]{3,2,0,1:T(8,128)} copy(f32[2,48,128,128]{3,2,1,0:T(8,128)} %scatter_fusion) | data formatting | bytes 12582912 | tf_op jit(solution)/shard_map/scatter | solution.py:51
  84.7 4.7 %all-to-all-start = ((f32[2,48,128,128]{3,2,0,1:T(8,128)}), f32[2,48,128,128]{3,2,0,1:T(8,128)}, u32[]{:S(2)}, u32[]{:S(2)}) async-start(f32[2,48,128,128]{3,2,0,1:T(8,128)} %copy.45), calls=%async_computation | async-start | bytes 12582912 | tf_op jit(solution)/shard_map/all_to_all | solution.py:52
  89.4 0.1 iota_add_fusion
  89.5 0.1 add.94
  89.6 0.2 select_reduce_fusion.1
  89.8 69.4 %all-to-all-done = f32[2,48,128,128]{3,2,0,1:T(8,128)} async-done(((f32[2,48,128,128]{3,2,0,1:T(8,128)}), f32[2,48,128,128]{3,2,0,1:T(8,128)}, u32[]{:S(2)}, u32[]{:S(2)}) %all-to-all-start) | async-done | bytes 6291488 | tf_op jit(solution)/shard_map/all_to_all | solution.py:52
  159.2 6.3 %copy.46 = f32[2,48,128,128]{3,2,1,0:T(8,128)} copy(f32[2,48,128,128]{3,2,0,1:T(8,128)} %all-to-all-done) | data formatting | bytes 12582912 | tf_op jit(solution)/shard_map/all_to_all | solution.py:52
  165.5 6.4 %gather_fusion = f32[48,2,128,128]{3,2,1,0:T(8,128)} fusion(f32[2,48,128,128]{3,2,1,0:T(8,128)} %copy.46, s32[1024]{0:T(1024)S(1)} %pad_clamp_fusion), kind=kCustom, calls=%fused_computation | custom fusion | bytes 12583104 | tf_op jit(solution)/shard_map/jit(_take)/gather | solution.py:61
  171.9 7.0 %select_bitcast_fusion = f32[2,48,128,128]{3,2,0,1:T(8,128)} fusion(f32[48,2,128,128]{3,2,1,0:T(8,128)} %gather_fusion, pred[48]{0:T(512)(128)(4,1)S(1)} %get-tuple-element.14, pred[48]{0:T(512)(128)(4,1)S(1)} %get-tuple-element.13), kind=kLoop, calls=%fused_computation.4 | loop fusion | flops 3145728 | bytes 12583008 | tf_op jit(solution)/shard_map/jit(_where)/select_n | solution.py:62
  178.9 5.7 %all-to-all-start.1 = ((f32[2,48,128,128]{3,2,0,1:T(8,128)}), f32[2,48,128,128]{3,2,0,1:T(8,128)}, u32[]{:S(2)}, u32[]{:S(2)}) async-start(f32[2,48,128,128]{3,2,0,1:T(8,128)} %select_bitcast_fusion), calls=%async_computation.1 | async-start | bytes 12582912 | tf_op jit(solution)/shard_map/all_to_all | solution.py:63
  185.2 138.3 %all-to-all-done.1 = f32[2,48,128,128]{3,2,0,1:T(8,128)} async-done(((f32[2,48,128,128]{3,2,0,1:T(8,128)}), f32[2,48,128,128]{3,2,0,1:T(8,128)}, u32[]{:S(2)}, u32[]{:S(2)}) %all-to-all-start.1) | async-done | bytes 6291488 | tf_op jit(solution)/shard_map/all_to_all | solution.py:63
  323.5 3.2 copy.47
  326.8 0.8 select_reduce_fusion
  327.5 0.1 broadcast_multiply_fusion
  327.6 3.2 copy.48
  330.8 3.7 %fusion = f32[8,1,12,128,128]{4,3,2,0,1:T(8,128)} fusion(f32[4,2,12,128,128]{4,3,2,1,0:T(8,128)S(1)} %copy.48, f32[12,128,128]{2,1,0:T(8,128)S(1)} %broadcast_multiply_fusion, pred[12]{0:T(512)(128)(4,1)S(1)} %iota_compare_fusion.2), kind=kLoop, calls=%fused_computation.3 | loop fusion | flops 3145728 | bytes 13369356 | tf_op jit(solution)/shard_map/sub | solution.py:66
  (12 shorter events, 0.2 us)
Async XLA Ops:
  28.1 32.4 %copy-start.2 = (s32[192]{0:T(256)S(1)}, s32[192]{0:T(256)}, u32[]{:S(2)}) copy-start(s32[192]{0:T(256)} %param.8) | copy-start | bytes 2308
  66.7 0.7 copy-start
  66.7 0.7 copy-start.1
  84.7 74.5 %all-to-all-start = ((f32[2,48,128,128]{3,2,0,1:T(8,128)}), f32[2,48,128,128]{3,2,0,1:T(8,128)}, u32[]{:S(2)}, u32[]{:S(2)}) async-start(f32[2,48,128,128]{3,2,0,1:T(8,128)} %copy.45), calls=%async_computation | async-start | bytes 12582912 | tf_op jit(solution)/shard_map/all_to_all | solution.py:52
  178.9 144.6 %all-to-all-start.1 = ((f32[2,48,128,128]{3,2,0,1:T(8,128)}), f32[2,48,128,128]{3,2,0,1:T(8,128)}, u32[]{:S(2)}, u32[]{:S(2)}) async-start(f32[2,48,128,128]{3,2,0,1:T(8,128)} %select_bitcast_fusion), calls=%async_computation.1 | async-start | bytes 12582912 | tf_op jit(solution)/shard_map/all_to_all | solution.py:63
where the time goes:
time: 337 us; the launch traced here: 335 us
  waiting for transfers between devices  208 us (62%)
  local copies, waits for them, and re-layouts  96.6 us (29%)
  other arithmetic  19 us (6%)
  starting transfers between devices  10.4 us (3%)
    all_to_all x1, waiting for transfers between devices, on_device(): lax.all_to_all(picked, 'gy', split_axis=1, concat_axis=0, tiled=True)  138 us
    all_to_all x1, waiting for transfers between devices, on_device(): lax.all_to_all(outgoing, 'gx', split_axis=1, concat_axis=1, tiled=True)  69.4 us
    rev x1, local copies, waits for them, and re-layouts, spin_patches(): half_turn = jnp.rot90(incoming_patches, 2, axes=(2, 3))  25.7 us
    rev x1, local copies, waits for them, and re-layouts, spin_patches(): last_turn = jnp.rot90(incoming_patches, 3, axes=(2, 3))  17 us
    rev x1, local copies, waits for them, and re-layouts, spin_patches(): first_turn = jnp.rot90(incoming_patches, 1, axes=(2, 3))  15.3 us
    scatter x2, local copies, waits for them, and re-layouts, on_device(): outgoing = outgoing.at[:, mine_place].set(incoming_patches)  12.7 us
    select_n x1, other arithmetic, on_device(): picked = jnp.where(present[None, :, None, None], picked, jnp.float32(0.0))  7.01 us
  transfers between devices with their start and end apart: 2, of which 2 were waited for; matrix products, arithmetic and copies ran while one was open for 0% of the time, Pallas kernels for 0%

commit v1 on v0

--- a/solution.py
+++ b/solution.py
@@ -25,6 +25,15 @@
 
 
 def on_device(ocean_heat_field, patch_zone, patch_position, quarter_spins, zone_patch_tally):
+
+    def launch_goods(point, shard_axis):
+        return jnp.concatenate(
+            jax.lax.all_to_all(
+                jnp.stack(jnp.split(point, jax.lax.axis_size(shard_axis), axis=1)), shard_axis, 0, 0
+            ),
+            axis=1,
+        )
+
     epoch_anomalies = ocean_heat_field.shape[0]
     patch_anomalies = ocean_heat_field.shape[1]
     patch_side_length = ocean_heat_field.shape[2]
@@ -49,7 +58,7 @@
         jnp.float32,
     )
     outgoing = outgoing.at[:, mine_place].set(incoming_patches)
-    arrived = lax.all_to_all(outgoing, "gx", split_axis=1, concat_axis=1, tiled=True)
+    arrived = launch_goods(outgoing, shard_axis="gx")
     arrival = source_group * per_peer + order_rank
     row_ids = jnp.arange(row_count, dtype=jnp.int32)[:, None]
     slot_ids = jnp.arange(capacity, dtype=jnp.int32)[None, :]

time: 337 us -> 348 us (1.033)
  local copies, waits for them, and re-layouts: 96.6 us -> 107 us
    unnamed x7 -> x14, local copies, waits for them, and re-layouts: 2.85 us -> 17.5 us
    reshape x0 -> x1, local copies, waits for them, and re-layouts: none -> 6.28 us  [launch_goods(): jnp.concatenate(jax.lax.all_to_all(jnp.stack(jnp.split(point, jax.lax.axi...]
    all_to_all x1 -> x0, local copies, waits for them, and re-layouts: 6.28 us -> none  [on_device(): lax.all_to_all(outgoing, 'gx', split_axis=1, concat_axis=1, tiled=True)]
    scatter x2 -> x1, local copies, waits for them, and re-layouts: 12.7 us -> 6.45 us  [on_device(): outgoing = outgoing.at[:, mine_place].set(incoming_patches)]
where the time goes in v1:
time: 348 us; the launch traced here: 345 us
  waiting for transfers between devices  208 us (60%)
  local copies, waits for them, and re-layouts  107 us (31%)
  other arithmetic  19 us (5%)
  starting transfers between devices  10.4 us (3%)
    all_to_all x1, waiting for transfers between devices, on_device(): lax.all_to_all(picked, 'gy', split_axis=1, concat_axis=0, tiled=True)  138 us
    all_to_all x1, waiting for transfers between devices, launch_goods(): jax.lax.all_to_all(jnp.stack(jnp.split(point, jax.lax.axis_size(shard_axi...  69.4 us
    rev x1, local copies, waits for them, and re-layouts, spin_patches(): half_turn = jnp.rot90(incoming_patches, 2, axes=(2, 3))  25.7 us
    unnamed x14, local copies, waits for them, and re-layouts  17.5 us
    rev x1, local copies, waits for them, and re-layouts, spin_patches(): last_turn = jnp.rot90(incoming_patches, 3, axes=(2, 3))  17 us
    rev x1, local copies, waits for them, and re-layouts, spin_patches(): first_turn = jnp.rot90(incoming_patches, 1, axes=(2, 3))  15.3 us
    select_n x1, other arithmetic, on_device(): picked = jnp.where(present[None, :, None, None], picked, jnp.float32(0.0))  7.01 us
  transfers between devices with their start and end apart: 2, of which 2 were waited for; matrix products, arithmetic and copies ran while one was open for 0% of the time, Pallas kernels for 0%

profile of v1, /device:TPU:2, one launch (start us, length us, event | category | flops | bytes accessed | tf_op | source)
XLA Modules:
  0.0 345.1 jit_solution(11223330677872682965)
XLA Ops:
  0.0 2.4 copy.26
  2.4 25.7 %rev.17 = f32[2,24,128,128]{3,2,1,0:T(8,128)} reverse(f32[2,24,128,128]{3,2,1,0:T(8,128)} %param.5), dimensions={2,3} | reverse | bytes 6291456 | tf_op jit(solution)/shard_map/jit(rot90)/jit(_flip)/rev | solution.py:9
  28.1 0.0 copy-start.2
  28.1 15.3 %rev.16 = f32[2,24,128,128]{2,3,1,0:T(8,128)} reverse(f32[2,24,128,128]{2,3,1,0:T(8,128)S(1)} %copy.26), dimensions={3} | reverse | bytes 6291456 | tf_op jit(solution)/shard_map/jit(rot90)/jit(_flip)/rev | solution.py:8
  43.4 17.0 %rev.18 = f32[2,24,128,128]{3,2,1,0:T(8,128)} reverse(f32[2,24,128,128]{3,2,1,0:T(8,128)S(1)} %bitcast.68), dimensions={3} | reverse | bytes 6291456 | tf_op jit(solution)/shard_map/jit(rot90)/jit(_flip)/rev | solution.py:10
  60.4 0.0 copy-done.2
  60.4 0.1 broadcast_compare_fusion.2
  60.5 6.2 %fusion.2 = f32[24,2,128,128]{3,2,0,1:T(8,128)S(1)} fusion(f32[2,24,128,128]{3,2,1,0:T(8,128)} %param.5, f32[2,24,128,128]{2,3,1,0:T(8,128)} %rev.16, f32[2,24,128,128]{3,2,1,0:T(8,128)} %rev.17, f32[2,24,128,128]{3,2,1,0:T(8,128)} %rev.18, pred[24]{0:T(512)(128)(4,1)S(1)} %get-tuple-element.12, pred[24]{0:T(512)(128)(4,1)S(1)} %get-tuple-element.11, ...), kind=kLoop, calls=%fused_computation.8 | loop fusion | flops 2359296 | bytes 15728712 | tf_op jit(solution)/shard_map/jit(_where)/select_n | solution.py:12
  66.7 0.0 copy-start
  66.7 0.0 copy-start.1
  66.7 0.2 copy.28
  66.9 0.4 copy-done
  67.4 0.0 copy-done.1
  67.4 0.6 reduce-window.6
  68.0 0.2 slice_reduce_fusion
  68.3 0.1 bitcast_bitcast_fusion
  68.4 0.1 compare_select_fusion
  68.5 3.5 %broadcast_in_dim.88 = f32[2,48,128,128]{3,2,1,0:T(8,128)} broadcast(f32[]{:T(128)} %constant.72.clone.1), dimensions={} | broadcast | bytes 6291460 | tf_op jit(solution)/shard_map/broadcast_in_dim | solution.py:56
  72.0 6.4 %scatter_fusion = f32[2,48,128,128]{3,2,1,0:T(8,128)} fusion(f32[2,48,128,128]{3,2,1,0:T(8,128)} %broadcast_in_dim.88, s32[24]{0:T(128)S(1)} %compare_select_fusion, f32[24,2,128,128]{3,2,1,0:T(8,128)S(1)} %copy.28), kind=kCustom, calls=%fused_computation.1 | custom fusion | bytes 9437280 | tf_op jit(solution)/shard_map/scatter | solution.py:60
  78.4 2.1 fusion.10
  80.5 2.1 fusion.9
  82.6 2.1 fusion.8
  84.7 2.2 fusion.7
  86.8 2.1 fusion.6
  88.9 2.1 fusion.5
  91.0 2.1 fusion.4
  93.1 2.1 fusion.3
  95.2 4.7 %all-to-all-start = ((f32[8,2,6,128,128]{4,3,2,1,0:T(8,128)}), f32[8,2,6,128,128]{4,3,2,1,0:T(8,128)}, u32[]{:S(2)}, u32[]{:S(2)}) async-start(f32[8,2,6,128,128]{4,3,2,1,0:T(8,128)} %fusion.3), calls=%async_computation | async-start | bytes 12582912 | tf_op jit(solution)/shard_map/all_to_all | solution.py:31
  99.9 0.1 iota_add_fusion
  100.0 0.1 add.94
  100.1 0.2 select_reduce_fusion.1
  100.3 69.4 %all-to-all-done = f32[8,2,6,128,128]{4,3,2,1,0:T(8,128)} async-done(((f32[8,2,6,128,128]{4,3,2,1,0:T(8,128)}), f32[8,2,6,128,128]{4,3,2,1,0:T(8,128)}, u32[]{:S(2)}, u32[]{:S(2)}) %all-to-all-start) | async-done | bytes 6291488 | tf_op jit(solution)/shard_map/all_to_all | solution.py:31
  169.7 6.3 %copy.29 = f32[2,8,6,128,128]{4,3,2,1,0:T(8,128)} copy(f32[2,8,6,128,128]{4,3,2,0,1:T(8,128)} %bitcast.13) | data formatting | bytes 12582912 | tf_op jit(solution)/shard_map/reshape | solution.py:30
  176.0 6.4 %gather_fusion = f32[48,2,128,128]{3,2,1,0:T(8,128)} fusion(f32[2,48,128,128]{3,2,1,0:T(8,128)} %bitcast.69, s32[1024]{0:T(1024)S(1)} %pad_clamp_fusion), kind=kCustom, calls=%fused_computation | custom fusion | bytes 12583104 | tf_op jit(solution)/shard_map/jit(_take)/gather | solution.py:70
  182.4 7.0 %select_bitcast_fusion = f32[2,48,128,128]{3,2,0,1:T(8,128)} fusion(f32[48,2,128,128]{3,2,1,0:T(8,128)} %gather_fusion, pred[48]{0:T(512)(128)(4,1)S(1)} %get-tuple-element.14, pred[48]{0:T(512)(128)(4,1)S(1)} %get-tuple-element.13), kind=kLoop, calls=%fused_computation.4 | loop fusion | flops 3145728 | bytes 12583008 | tf_op jit(solution)/shard_map/jit(_where)/select_n | solution.py:71
  189.4 5.7 %all-to-all-start.1 = ((f32[2,48,128,128]{3,2,0,1:T(8,128)}), f32[2,48,128,128]{3,2,0,1:T(8,128)}, u32[]{:S(2)}, u32[]{:S(2)}) async-start(f32[2,48,128,128]{3,2,0,1:T(8,128)} %select_bitcast_fusion), calls=%async_computation.1 | async-start | bytes 12582912 | tf_op jit(solution)/shard_map/all_to_all | solution.py:72
  195.7 138.3 %all-to-all-done.1 = f32[2,48,128,128]{3,2,0,1:T(8,128)} async-done(((f32[2,48,128,128]{3,2,0,1:T(8,128)}), f32[2,48,128,128]{3,2,0,1:T(8,128)}, u32[]{:S(2)}, u32[]{:S(2)}) %all-to-all-start.1) | async-done | bytes 6291488 | tf_op jit(solution)/shard_map/all_to_all | solution.py:72
  334.0 3.2 copy.30
  337.2 0.8 select_reduce_fusion
  338.0 0.1 broadcast_multiply_fusion
  338.1 3.2 copy.31
  341.3 3.7 %fusion = f32[8,1,12,128,128]{4,3,2,0,1:T(8,128)} fusion(f32[4,2,12,128,128]{4,3,2,1,0:T(8,128)S(1)} %copy.31, f32[12,128,128]{2,1,0:T(8,128)S(1)} %broadcast_multiply_fusion, pred[12]{0:T(512)(128)(4,1)S(1)} %iota_compare_fusion.2), kind=kLoop, calls=%fused_computation.3 | loop fusion | flops 3145728 | bytes 13369356 | tf_op jit(solution)/shard_map/sub | solution.py:75
  (12 shorter events, 0.2 us)
Async XLA Ops:
  28.1 32.4 %copy-start.2 = (s32[192]{0:T(256)S(1)}, s32[192]{0:T(256)}, u32[]{:S(2)}) copy-start(s32[192]{0:T(256)} %param.8) | copy-start | bytes 2308
  66.7 0.7 copy-start
  66.7 0.7 copy-start.1
  95.2 74.5 %all-to-all-start = ((f32[8,2,6,128,128]{4,3,2,1,0:T(8,128)}), f32[8,2,6,128,128]{4,3,2,1,0:T(8,128)}, u32[]{:S(2)}, u32[]{:S(2)}) async-start(f32[8,2,6,128,128]{4,3,2,1,0:T(8,128)} %fusion.3), calls=%async_computation | async-start | bytes 12582912 | tf_op jit(solution)/shard_map/all_to_all | solution.py:31
  189.4 144.6 %all-to-all-start.1 = ((f32[2,48,128,128]{3,2,0,1:T(8,128)}), f32[2,48,128,128]{3,2,0,1:T(8,128)}, u32[]{:S(2)}, u32[]{:S(2)}) async-start(f32[2,48,128,128]{3,2,0,1:T(8,128)} %select_bitcast_fusion), calls=%async_computation.1 | async-start | bytes 12582912 | tf_op jit(solution)/shard_map/all_to_all | solution.py:72
